TPU v7x, 64 devices: a 2x2x8 block of a 4x4x8 slice. The times are simulated.
64 devices in a mesh: rep: 8 (over x, y, core), dp: 8 (over z).
Axes of the slice: x: 2, y: 2, z: 8, core: 2. Of those that a mesh axis runs over, the one named last changes fastest.
The devices are a block of a 4x4x8 slice.
Arguments:
- a: bfloat16 [64, 4, 4096, 896], P(('rep', 'dp')), parts along dimension 0
- g: bfloat16 [64, 4, 4096, 2560], P(('rep', 'dp')), parts along dimension 0
Outputs:
- output: bfloat16 [32, 896, 2560], P('rep'), parts along dimension 0
There are 8 independent parts. A program takes and returns all parts, laid end to end along the dimension named above; each array names one.
All inputs are finite; a program needn't handle non-finite values.
Results may differ from a plain program's by a relative error of at most 0.012.
Values are sent between devices in bfloat16 or wider.
A program may use at most 768 MiB of HBM per device.

v0:
```python
import jax
import jax.numpy as jnp


def solution(mesh):
    groups = mesh.shape["rep"]

    def step(a, g):
        a, g = (t.reshape(groups, -1, *t.shape[1:]) for t in (a, g))
        sums = jnp.einsum("rsntd,rsntf->rndf", a, g, preferred_element_type=jnp.float32)
        return sums.astype(jnp.bfloat16).reshape(-1, *sums.shape[2:])

    return step
```

profile of v0, /device:TPU:21, one launch (start us, length us, event | category | flops | bytes accessed | tf_op | source)
XLA Modules:
  0.0 803.0 jit_solution(4262067998814600122)
XLA Ops:
  0.0 87.3 %fusion.3 = f32[1,4,896,2560]{3,2,1,0:T(8,128)} fusion(bf16[1,4,4096,2560]{3,2,1,0:T(8,128)(2,1)} %param.1, bf16[1,4,4096,896]{3,2,1,0:T(8,128)(2,1)} %param), kind=kOutput, calls=%fused_computation.3 | convolution fusion | flops 75161927680 | bytes 149946368 | tf_op jit(solution)/rsntd,rsntf->rndf/dot_general | solution.py:10
  87.3 715.7 %all-reduce.2 = bf16[1,4,896,2560]{3,2,1,0:T(8,128)(2,1)} all-reduce(f32[1,4,896,2560]{3,2,1,0:T(8,128)} %fusion.3), channel_id=1, replica_groups=[8,8]<=[64], use_global_device_ids=true, to_apply=%add.clone | all-reduce | flops 9175040 | bytes 55050240 | tf_op jit(solution)/rsntd,rsntf->rndf/dot_general | solution.py:10
where the time goes:
time: 804 us; the launch traced here: 803 us
  blocking collectives  716 us (89%)
  matrix products  87.3 us (11%)
    dot_general x1, blocking collectives, step(): jnp.einsum('rsntd,rsntf->rndf', a, g, preferred_element_type=jnp.float32)  716 us
    dot_general x1, matrix products, step(): jnp.einsum('rsntd,rsntf->rndf', a, g, preferred_element_type=jnp.float32)  87.3 us

commit v1 on v0

v1 whole, which is shorter than its diff:
```python
import functools

import jax
import jax.numpy as jnp
from jax import lax
from jax.experimental import pallas as pl
from jax.experimental.pallas import tpu as pltpu
from jax.sharding import PartitionSpec as P

COLS = 256
LANES = 128
A_SLOTS = 3
G_SLOTS = 3
P_SLOTS = 2
SEMS = 8


class Plan:
    def __init__(self, ring, matrices, tokens, rows, cols):
        self.ring, self.matrices, self.tokens, self.rows, self.cols = ring, matrices, tokens, rows, cols
        self.per_matrix = cols // COLS
        self.units = matrices * self.per_matrix
        self.sets = self.units // ring
        assert self.sets * ring == self.units and self.sets >= 3
        self.half = rows // 2
        self.span = -(-self.half // LANES) * LANES
        self.phase = 2 * (ring - 1)
        self.slots = self.sets * self.phase

    def final_slot(self, s):
        return (self.phase + 1 + 2 * s) if s < 2 else s * self.phase + 1

    def first_slot(self, s):
        return s if s < 2 else (s - 1) * self.phase

    def load_slot(self, m):
        last = (m - A_SLOTS + 1) * self.per_matrix - 1
        return self.final_slot(last // self.ring) + 1

    def need_slot(self, m):
        return self.first_slot(m * self.per_matrix // self.ring)

    def at(self, n):
        p, q = n // self.phase, n % self.phase
        b, k = q % 2, q // 2
        first, last = p == 0, p == self.sets - 1
        s_a = jnp.where(first, 0, jnp.where(last, self.sets - 2, p + 1))
        s_b = jnp.where(first, 1, jnp.where(last, self.sets - 1, p - 1))
        s = jnp.where(b == 0, s_a, s_b)
        scatter = jnp.logical_or(first, jnp.logical_and(b == 0, jnp.logical_not(last)))
        return s, k, scatter

    def final(self, n):
        ends, which = False, 0
        for s in range(self.sets):
            hit = n == self.final_slot(s)
            ends = jnp.logical_or(ends, hit)
            which = jnp.where(hit, s, which)
        return ends, which

    def job(self, n):
        s, k, scatter = self.at(n)
        ends, which = self.final(n)
        has = jnp.logical_and(jnp.logical_or(scatter, ends), n < self.slots)
        return has, jnp.where(ends, which, s), jnp.where(ends, self.ring - 1, k)


def reduce_kernel(plan, axis, a_ref, g_ref, x_ref, a_buf, g_buf, prod, a_sem, g_sem, send_sem, recv_sem):
    ring = plan.ring
    me = lax.axis_index(axis)
    neighbours = (lax.rem(me + 1, ring), lax.rem(me + ring - 1, ring))
    row0 = (0, plan.half)
    lane0 = (0, plan.rows - plan.span)

    barrier = pltpu.get_barrier_semaphore()
    for there in neighbours:
        pl.semaphore_signal(barrier, inc=1, device_id={axis: there}, device_id_type=pl.DeviceIdType.MESH)

    def chunk(d, k, scatter):
        hop = k + jnp.where(scatter, 1, 0)
        return lax.rem(me + (ring - hop if d == 0 else hop), ring)

    def job_unit(d, s, k):
        return s * ring + chunk(d, k, True)

    def block(u, d):
        return x_ref.at[u, pl.ds(row0[d], plan.half), :]

    def a_load(m):
        return pltpu.make_async_copy(a_ref.at[0, m], a_buf.at[m % A_SLOTS], a_sem.at[m % A_SLOTS])

    def g_load(d, u, n):
        m, j = u // plan.per_matrix, lax.rem(u, plan.per_matrix)
        slot = lax.rem(n, G_SLOTS)
        src = g_ref.at[0, m, :, pl.ds(pl.multiple_of(j * COLS, COLS), COLS)]
        return pltpu.make_async_copy(src, g_buf.at[d, slot], g_sem.at[d, slot])

    def fetch(n):
        has, s, k = plan.job(n)

        @pl.when(has)
        def _():
            for d in (0, 1):
                g_load(d, job_unit(d, s, k), n).start()

    def multiply(n):
        has, s, k = plan.job(n)

        @pl.when(has)
        def _():
            for d in (0, 1):
                u = job_unit(d, s, k)
                g_load(d, u, n).wait()
                prod[d, lax.rem(n, P_SLOTS)] = lax.dot_general(
                    a_buf[lax.rem(u // plan.per_matrix, A_SLOTS), :, pl.ds(lane0[d], plan.span)],
                    g_buf[d, lax.rem(n, G_SLOTS)],
                    (((0,), (0,)), ((), ())),
                    preferred_element_type=jnp.float32,
                )

    def add_product(d, n, u, fresh):
        off = row0[d] - lane0[d]
        mine = prod[d, lax.rem(n, P_SLOTS), pl.ds(off, plan.half), :]

        @pl.when(fresh)
        def _():
            x_ref[u, pl.ds(row0[d], plan.half), :] = mine.astype(x_ref.dtype)

        @pl.when(jnp.logical_not(fresh))
        def _():
            so_far = x_ref[u, pl.ds(row0[d], plan.half), :].astype(jnp.float32)
            x_ref[u, pl.ds(row0[d], plan.half), :] = (so_far + mine).astype(x_ref.dtype)

    def remote(d, u, n):
        i = lax.rem(n, SEMS)
        return pltpu.make_async_remote_copy(
            src_ref=block(u, d),
            dst_ref=block(u, d),
            send_sem=send_sem.at[d, i],
            recv_sem=recv_sem.at[d, i],
            device_id={axis: neighbours[d]},
            device_id_type=pl.DeviceIdType.MESH,
        )

    def turn(n):
        s, k, scatter = plan.at(n)
        has, js, jk = plan.job(n)
        for d in (0, 1):

            @pl.when(n >= 2)
            def _():
                remote(d, 0, n - 2 + SEMS).wait_recv()

            @pl.when(has)
            def _():
                add_product(d, n, job_unit(d, js, jk), jk == 0)

            @pl.when(n >= SEMS)
            def _():
                remote(d, 0, n).wait_send()

            remote(d, s * ring + chunk(d, k, scatter), n).start()

    first = range(min(A_SLOTS, plan.matrices))
    a_load(0).start()
    fetch(0)
    fetch(1)
    for m in first[1:]:
        a_load(m).start()
    fetch(2)
    a_load(0).wait()
    multiply(0)
    pl.semaphore_wait(barrier, 2)

    def body(n, _):
        turn(n)
        for m in range(1, plan.matrices):
            if m >= A_SLOTS:

                @pl.when(n == plan.load_slot(m))
                def _():
                    a_load(m).start()

            @pl.when(n + 1 == plan.need_slot(m))
            def _():
                a_load(m).wait()

        multiply(n + 1)
        fetch(n + 3)
        return 0

    lax.fori_loop(0, plan.slots, body, 0)
    for n in range(plan.slots - 2, plan.slots):
        for d in (0, 1):
            remote(d, 0, n).wait_recv()
    for n in range(plan.slots - SEMS, plan.slots):
        for d in (0, 1):
            remote(d, 0, n).wait_send()


def write_kernel(plan, x_ref, out_ref, sem):
    copies = []
    for u in range(plan.units):
        m, j = divmod(u, plan.per_matrix)
        copies.append(pltpu.make_async_copy(x_ref.at[u], out_ref.at[m, :, pl.ds(j * COLS, COLS)], sem.at[u]))
    for c in copies:
        c.start()
    for c in copies:
        c.wait()


def solution(mesh):
    axis = "dp"

    def device(a, g):
        _, matrices, tokens, rows = a.shape
        cols = g.shape[-1]
        plan = Plan(mesh.shape[axis], matrices, tokens, rows, cols)
        sums = pl.pallas_call(
            functools.partial(reduce_kernel, plan, axis),
            out_shape=pltpu.VMEM((plan.units, rows, COLS), jnp.bfloat16),
            in_specs=[pl.BlockSpec(memory_space=pl.ANY)] * 2,
            out_specs=pl.BlockSpec(memory_space=pltpu.VMEM),
            scratch_shapes=[
                pltpu.VMEM((A_SLOTS, tokens, rows), jnp.bfloat16),
                pltpu.VMEM((2, G_SLOTS, tokens, COLS), jnp.bfloat16),
                pltpu.VMEM((2, P_SLOTS, plan.span, COLS), jnp.float32),
                pltpu.SemaphoreType.DMA((A_SLOTS,)),
                pltpu.SemaphoreType.DMA((2, G_SLOTS)),
                pltpu.SemaphoreType.DMA((2, SEMS)),
                pltpu.SemaphoreType.DMA((2, SEMS)),
            ],
            compiler_params=pltpu.CompilerParams(
                collective_id=0, has_side_effects=True, vmem_limit_bytes=44 * 2**20
            ),
            name="ring_sums",
        )(a, g)
        return pl.pallas_call(
            functools.partial(write_kernel, plan),
            out_shape=jax.ShapeDtypeStruct((matrices, rows, cols), jnp.bfloat16),
            in_specs=[pl.BlockSpec(memory_space=pltpu.VMEM)],
            out_specs=pl.BlockSpec(memory_space=pl.ANY),
            scratch_shapes=[pltpu.SemaphoreType.DMA((plan.units,))],
            compiler_params=pltpu.CompilerParams(vmem_limit_bytes=2**20),
            name="write_sums",
        )(pltpu.with_memory_space_constraint(sums, pltpu.VMEM))

    spec = P(("rep", axis))
    return jax.shard_map(device, mesh=mesh, in_specs=(spec, spec), out_specs=P("rep"), check_vma=False)
```

time: 804 us -> 370 us (0.46)
  blocking collectives: 716 us -> 0 us
  Pallas kernels: 0 us -> 370 us
  matrix products: 87.3 us -> 0 us
    dot_general x1 -> x0, blocking collectives: 716 us -> none  [step(): jnp.einsum('rsntd,rsntf->rndf', a, g, preferred_element_type=jnp.float32)]
    pallas_call x0 -> x2, Pallas kernels: none -> 370 us  [the longest x1 363 us: device(): pl.pallas_call(functools.partial(reduce_kernel, plan, axis), out_shape=pl...]
    dot_general x1 -> x0, matrix products: 87.3 us -> none  [step(): jnp.einsum('rsntd,rsntf->rndf', a, g, preferred_element_type=jnp.float32)]
where the time goes in v1:
time: 370 us
  Pallas kernels  370 us (100%)
    pallas_call x1, Pallas kernels, device(): pl.pallas_call(functools.partial(reduce_kernel, plan, axis), out_shape=pl...  363 us

profile of v1, /device:TPU:21, one launch (start us, length us, event | category | flops | bytes accessed | tf_op | source)
XLA Modules:
  0.0 369.7 jit_solution(8976560945382148906)
XLA Ops:
  0.0 363.0 %ring_sums.1.x_ref = bf16[40,896,256]{2,1,0:T(8,128)(2,1)S(1)} custom-call(bf16[1,4,4096,896]{3,2,1,0:T(8,128)(2,1)} %a_ref.1, bf16[1,4,4096,2560]{3,2,1,0:T(8,128)(2,1)} %g_ref.1), custom_call_target="tpu_custom_call" | custom-call | tf_op jit(solution)/shard_map/ring_sums/pallas_call | solution.py:219
  363.0 6.6 %write_sums.1 = bf16[4,896,2560]{2,1,0:T(8,128)(2,1)} custom-call(bf16[40,896,256]{2,1,0:T(8,128)(2,1)S(1)} %ring_sums.1.x_ref), custom_call_target="tpu_custom_call" | custom-call | tf_op jit(solution)/shard_map/write_sums/pallas_call | solution.py:238

commit v2 on v1

--- a/solution.py
+++ b/solution.py
@@ -11,8 +11,14 @@
 LANES = 128
 A_SLOTS = 3
 G_SLOTS = 3
+PIECES = 4
 P_SLOTS = 2
 SEMS = 8
+WRITES = 4
+
+
+def dot(a, g):
+    return lax.dot_general(a, g, (((0,), (0,)), ((), ())), preferred_element_type=jnp.float32)
 
 
 class Plan:
@@ -34,6 +40,8 @@
         return s if s < 2 else (s - 1) * self.phase
 
     def load_slot(self, m):
+        if m < A_SLOTS:
+            return m
         last = (m - A_SLOTS + 1) * self.per_matrix - 1
         return self.final_slot(last // self.ring) + 1
 
@@ -65,7 +73,7 @@
         return has, jnp.where(ends, which, s), jnp.where(ends, self.ring - 1, k)
 
 
-def reduce_kernel(plan, axis, a_ref, g_ref, x_ref, a_buf, g_buf, prod, a_sem, g_sem, send_sem, recv_sem):
+def reduce_kernel(plan, axis, a_ref, g_ref, x_ref, a_buf, g_buf, prod, a_sem, g_sem, send_sem, recv_sem, first_sem):
     ring = plan.ring
     me = lax.axis_index(axis)
     neighbours = (lax.rem(me + 1, ring), lax.rem(me + ring - 1, ring))
@@ -78,30 +86,40 @@
 
     def chunk(d, k, scatter):
         hop = k + jnp.where(scatter, 1, 0)
-        return lax.rem(me + (ring - hop if d == 0 else hop), ring)
+        return lax.rem(me + (ring - hop if d == 0 else ring - 2 + hop), ring)
+
+    def shared(k):
+        return lax.rem(2 * k, ring) == 0
 
     def job_unit(d, s, k):
         return s * ring + chunk(d, k, True)
 
+    def columns(u):
+        j = lax.rem(u, plan.per_matrix)
+        return u // plan.per_matrix, pl.ds(pl.multiple_of(j * COLS, COLS), COLS)
+
     def block(u, d):
-        return x_ref.at[u, pl.ds(row0[d], plan.half), :]
+        m, cols = columns(u)
+        return x_ref.at[m, pl.ds(row0[d], plan.half), cols]
 
     def a_load(m):
         return pltpu.make_async_copy(a_ref.at[0, m], a_buf.at[m % A_SLOTS], a_sem.at[m % A_SLOTS])
 
     def g_load(d, u, n):
-        m, j = u // plan.per_matrix, lax.rem(u, plan.per_matrix)
+        m, cols = columns(u)
         slot = lax.rem(n, G_SLOTS)
-        src = g_ref.at[0, m, :, pl.ds(pl.multiple_of(j * COLS, COLS), COLS)]
-        return pltpu.make_async_copy(src, g_buf.at[d, slot], g_sem.at[d, slot])
+        return pltpu.make_async_copy(g_ref.at[0, m, :, cols], g_buf.at[d, slot], g_sem.at[d, slot])
 
     def fetch(n):
         has, s, k = plan.job(n)
 
         @pl.when(has)
         def _():
-            for d in (0, 1):
-                g_load(d, job_unit(d, s, k), n).start()
+            g_load(0, job_unit(0, s, k), n).start()
+
+        @pl.when(jnp.logical_and(has, jnp.logical_not(shared(k))))
+        def _():
+            g_load(1, job_unit(1, s, k), n).start()
 
     def multiply(n):
         has, s, k = plan.job(n)
@@ -110,26 +128,60 @@
         def _():
             for d in (0, 1):
                 u = job_unit(d, s, k)
-                g_load(d, u, n).wait()
-                prod[d, lax.rem(n, P_SLOTS)] = lax.dot_general(
+                if d == 0:
+                    g_load(0, u, n).wait()
+                else:
+
+                    @pl.when(jnp.logical_not(shared(k)))
+                    def _():
+                        g_load(1, u, n).wait()
+
+                from_buf = 0 if d == 0 else jnp.where(shared(k), 0, 1)
+                prod[d, lax.rem(n, P_SLOTS)] = dot(
                     a_buf[lax.rem(u // plan.per_matrix, A_SLOTS), :, pl.ds(lane0[d], plan.span)],
-                    g_buf[d, lax.rem(n, G_SLOTS)],
-                    (((0,), (0,)), ((), ())),
-                    preferred_element_type=jnp.float32,
+                    g_buf[from_buf, lax.rem(n, G_SLOTS)],
                 )
+
+    piece = plan.tokens // PIECES
+    splits = ((0, plan.span), (plan.span, plan.rows - plan.span))
+
+    def first_a(d, i):
+        toks, lanes = pl.ds(i * piece, piece), pl.ds(*splits[d])
+        return pltpu.make_async_copy(a_ref.at[0, 0, toks, lanes], a_buf.at[0, toks, lanes], first_sem.at[d, i])
+
+    def first_g(i):
+        toks, (m, cols) = pl.ds(i * piece, piece), columns(job_unit(0, 0, 0))
+        return pltpu.make_async_copy(g_ref.at[0, m, toks, cols], g_buf.at[0, 0, toks], first_sem.at[2, i])
+
+    def first_product(d):
+        for i in range(PIECES):
+            first_a(d, i).wait()
+            if d == 0:
+                first_g(i).wait()
+            toks = pl.ds(i * piece, piece)
+            part = dot(a_buf[0, toks, pl.ds(lane0[d], plan.span)], g_buf[0, 0, toks])
+            if i == 0:
+                prod[d, 0] = part
+            else:
+                prod[d, 0] += part
 
     def add_product(d, n, u, fresh):
         off = row0[d] - lane0[d]
         mine = prod[d, lax.rem(n, P_SLOTS), pl.ds(off, plan.half), :]
+        m, cols = columns(u)
+        there = (m, pl.ds(row0[d], plan.half), cols)
+
+        if fresh is True:
+            x_ref[there] = mine.astype(x_ref.dtype)
+            return
 
         @pl.when(fresh)
         def _():
-            x_ref[u, pl.ds(row0[d], plan.half), :] = mine.astype(x_ref.dtype)
+            x_ref[there] = mine.astype(x_ref.dtype)
 
         @pl.when(jnp.logical_not(fresh))
         def _():
-            so_far = x_ref[u, pl.ds(row0[d], plan.half), :].astype(jnp.float32)
-            x_ref[u, pl.ds(row0[d], plan.half), :] = (so_far + mine).astype(x_ref.dtype)
+            x_ref[there] = (x_ref[there].astype(jnp.float32) + mine).astype(x_ref.dtype)
 
     def remote(d, u, n):
         i = lax.rem(n, SEMS)
@@ -142,40 +194,32 @@
             device_id_type=pl.DeviceIdType.MESH,
         )
 
-    def turn(n):
+    def turn_one(d, n):
         s, k, scatter = plan.at(n)
         has, js, jk = plan.job(n)
-        for d in (0, 1):
-
-            @pl.when(n >= 2)
-            def _():
-                remote(d, 0, n - 2 + SEMS).wait_recv()
-
-            @pl.when(has)
-            def _():
-                add_product(d, n, job_unit(d, js, jk), jk == 0)
-
-            @pl.when(n >= SEMS)
-            def _():
-                remote(d, 0, n).wait_send()
-
-            remote(d, s * ring + chunk(d, k, scatter), n).start()
-
-    first = range(min(A_SLOTS, plan.matrices))
-    a_load(0).start()
-    fetch(0)
-    fetch(1)
-    for m in first[1:]:
-        a_load(m).start()
-    fetch(2)
-    a_load(0).wait()
-    multiply(0)
-    pl.semaphore_wait(barrier, 2)
-
-    def body(n, _):
-        turn(n)
+
+        @pl.when(n >= 2)
+        def _():
+            remote(d, 0, n - 2 + SEMS).wait_recv()
+
+        @pl.when(has)
+        def _():
+            add_product(d, n, job_unit(d, js, jk), jk == 0)
+
+        @pl.when(n >= SEMS)
+        def _():
+            remote(d, 0, n).wait_send()
+
+        remote(d, s * ring + chunk(d, k, scatter), n).start()
+
+    def first_turn(d):
+        u = job_unit(d, 0, 0)
+        add_product(d, 0, u, True)
+        remote(d, u, 0).start()
+
+    def multiply_next(n):
         for m in range(1, plan.matrices):
-            if m >= A_SLOTS:
+            if m >= 2:
 
                 @pl.when(n == plan.load_slot(m))
                 def _():
@@ -186,10 +230,32 @@
                 a_load(m).wait()
 
         multiply(n + 1)
+
+    for i in range(PIECES):
+        first_a(0, i).start()
+        first_g(i).start()
+    for i in range(PIECES):
+        first_a(1, i).start()
+    fetch(1)
+    if plan.matrices > 1:
+        a_load(1).start()
+    first_product(0)
+    pl.semaphore_wait(barrier, 2)
+    first_turn(0)
+    first_product(1)
+    first_turn(1)
+    fetch(2)
+    multiply_next(0)
+    fetch(3)
+
+    def body(n, _):
+        for d in (0, 1):
+            turn_one(d, n)
+        multiply_next(n)
         fetch(n + 3)
         return 0
 
-    lax.fori_loop(0, plan.slots, body, 0)
+    lax.fori_loop(1, plan.slots, body, 0)
     for n in range(plan.slots - 2, plan.slots):
         for d in (0, 1):
             remote(d, 0, n).wait_recv()
@@ -198,11 +264,13 @@
             remote(d, 0, n).wait_send()
 
 
-def write_kernel(plan, x_ref, out_ref, sem):
+def write_kernel(pieces, x_ref, out_ref, sem):
+    matrices, rows, _ = x_ref.shape
+    tall = rows // pieces
     copies = []
-    for u in range(plan.units):
-        m, j = divmod(u, plan.per_matrix)
-        copies.append(pltpu.make_async_copy(x_ref.at[u], out_ref.at[m, :, pl.ds(j * COLS, COLS)], sem.at[u]))
+    for i in range(matrices * pieces):
+        at = (i // pieces, pl.ds(i % pieces * tall, tall))
+        copies.append(pltpu.make_async_copy(x_ref.at[at], out_ref.at[at], sem.at[i]))
     for c in copies:
         c.start()
     for c in copies:
@@ -218,7 +286,7 @@
         plan = Plan(mesh.shape[axis], matrices, tokens, rows, cols)
         sums = pl.pallas_call(
             functools.partial(reduce_kernel, plan, axis),
-            out_shape=pltpu.VMEM((plan.units, rows, COLS), jnp.bfloat16),
+            out_shape=pltpu.VMEM((matrices, rows, cols), jnp.bfloat16),
             in_specs=[pl.BlockSpec(memory_space=pl.ANY)] * 2,
             out_specs=pl.BlockSpec(memory_space=pltpu.VMEM),
             scratch_shapes=[
@@ -229,6 +297,7 @@
                 pltpu.SemaphoreType.DMA((2, G_SLOTS)),
                 pltpu.SemaphoreType.DMA((2, SEMS)),
                 pltpu.SemaphoreType.DMA((2, SEMS)),
+                pltpu.SemaphoreType.DMA((3, PIECES)),
             ],
             compiler_params=pltpu.CompilerParams(
                 collective_id=0, has_side_effects=True, vmem_limit_bytes=44 * 2**20
@@ -236,11 +305,11 @@
             name="ring_sums",
         )(a, g)
         return pl.pallas_call(
-            functools.partial(write_kernel, plan),
+            functools.partial(write_kernel, WRITES),
             out_shape=jax.ShapeDtypeStruct((matrices, rows, cols), jnp.bfloat16),
             in_specs=[pl.BlockSpec(memory_space=pltpu.VMEM)],
             out_specs=pl.BlockSpec(memory_space=pl.ANY),
-            scratch_shapes=[pltpu.SemaphoreType.DMA((plan.units,))],
+            scratch_shapes=[pltpu.SemaphoreType.DMA((matrices * WRITES,))],
             compiler_params=pltpu.CompilerParams(vmem_limit_bytes=2**20),
             name="write_sums",
         )(pltpu.with_memory_space_constraint(sums, pltpu.VMEM))

time: 370 us -> 365 us (0.986)
  Pallas kernels: 370 us -> 365 us
    pallas_call x1, Pallas kernels: 363 us -> 359 us  [device(): pl.pallas_call(functools.partial(reduce_kernel, plan, axis), out_shape=pl...]
where the time goes in v2:
time: 365 us
  Pallas kernels  365 us (100%)
    pallas_call x1, Pallas kernels, device(): pl.pallas_call(functools.partial(reduce_kernel, plan, axis), out_shape=pl...  359 us

profile of v2, /device:TPU:21, one launch (start us, length us, event | category | flops | bytes accessed | tf_op | source)
XLA Modules:
  0.0 365.2 jit_solution(15423565219661569112)
XLA Ops:
  0.0 358.7 %ring_sums.1.x_ref = bf16[4,896,2560]{2,1,0:T(8,128)(2,1)S(1)} custom-call(bf16[1,4,4096,896]{3,2,1,0:T(8,128)(2,1)} %a_ref.1, bf16[1,4,4096,2560]{3,2,1,0:T(8,128)(2,1)} %g_ref.1), custom_call_target="tpu_custom_call" | custom-call | tf_op jit(solution)/shard_map/ring_sums/pallas_call | solution.py:287
  358.8 6.4 %write_sums.1 = bf16[4,896,2560]{2,1,0:T(8,128)(2,1)} custom-call(bf16[4,896,2560]{2,1,0:T(8,128)(2,1)S(1)} %ring_sums.1.x_ref), custom_call_target="tpu_custom_call" | custom-call | tf_op jit(solution)/shard_map/write_sums/pallas_call | solution.py:307

commit v3 on v2

--- a/solution.py
+++ b/solution.py
@@ -28,10 +28,17 @@
         self.units = matrices * self.per_matrix
         self.sets = self.units // ring
         assert self.sets * ring == self.units and self.sets >= 3
+        assert matrices >= 2 and self.per_matrix % 2 == 0 and self.per_matrix >= ring > self.per_matrix // 2
         self.half = rows // 2
+        self.quick = -(-self.half // (2 * LANES)) * LANES
         self.span = -(-self.half // LANES) * LANES
         self.phase = 2 * (ring - 1)
         self.slots = self.sets * self.phase
+
+    def unit(self, s, c):
+        h = self.per_matrix // 2
+        pair = jnp.where(c < h, c + h * s, self.per_matrix + c - h + (self.ring - h) * s)
+        return jnp.where(s < 2, pair, s * self.ring + c)
 
     def final_slot(self, s):
         return (self.phase + 1 + 2 * s) if s < 2 else s * self.phase + 1
@@ -43,10 +50,17 @@
         if m < A_SLOTS:
             return m
         last = (m - A_SLOTS + 1) * self.per_matrix - 1
-        return self.final_slot(last // self.ring) + 1
+        return self.final_slot(max(last // self.ring, 1)) + 1
 
     def need_slot(self, m):
         return self.first_slot(m * self.per_matrix // self.ring)
+
+    def columns(self, u):
+        j = lax.rem(u, self.per_matrix)
+        return u // self.per_matrix, pl.ds(pl.multiple_of(j * COLS, COLS), COLS)
+
+    def chunk(self, me, d, hop):
+        return lax.rem(me + (self.ring - hop if d == 0 else self.ring - 2 + hop), self.ring)
 
     def at(self, n):
         p, q = n // self.phase, n % self.phase
@@ -73,7 +87,7 @@
         return has, jnp.where(ends, which, s), jnp.where(ends, self.ring - 1, k)
 
 
-def reduce_kernel(plan, axis, a_ref, g_ref, x_ref, a_buf, g_buf, prod, a_sem, g_sem, send_sem, recv_sem, first_sem):
+def reduce_kernel(plan, axis, a_ref, g_ref, x_ref, a_buf, g_buf, prod, a_sem, g_sem, send_sem, recv_sem, first_sem, first_send, first_recv):
     ring = plan.ring
     me = lax.axis_index(axis)
     neighbours = (lax.rem(me + 1, ring), lax.rem(me + ring - 1, ring))
@@ -85,18 +99,15 @@
         pl.semaphore_signal(barrier, inc=1, device_id={axis: there}, device_id_type=pl.DeviceIdType.MESH)
 
     def chunk(d, k, scatter):
-        hop = k + jnp.where(scatter, 1, 0)
-        return lax.rem(me + (ring - hop if d == 0 else ring - 2 + hop), ring)
+        return plan.chunk(me, d, k + jnp.where(scatter, 1, 0))
 
     def shared(k):
         return lax.rem(2 * k, ring) == 0
 
     def job_unit(d, s, k):
-        return s * ring + chunk(d, k, True)
-
-    def columns(u):
-        j = lax.rem(u, plan.per_matrix)
-        return u // plan.per_matrix, pl.ds(pl.multiple_of(j * COLS, COLS), COLS)
+        return plan.unit(s, chunk(d, k, True))
+
+    columns = plan.columns
 
     def block(u, d):
         m, cols = columns(u)
@@ -142,38 +153,66 @@
                     g_buf[from_buf, lax.rem(n, G_SLOTS)],
                 )
 
-    piece = plan.tokens // PIECES
-    splits = ((0, plan.span), (plan.span, plan.rows - plan.span))
-
-    def first_a(d, i):
-        toks, lanes = pl.ds(i * piece, piece), pl.ds(*splits[d])
-        return pltpu.make_async_copy(a_ref.at[0, 0, toks, lanes], a_buf.at[0, toks, lanes], first_sem.at[d, i])
+    piece, quick = plan.tokens // PIECES, plan.quick
+    first_unit = job_unit(0, 0, 0)
+    first_m = first_unit // plan.per_matrix
+    other_m = 1 - first_m
+    parts = (
+        (0, (0, quick), (0, quick), (0, quick)),
+        (1, (plan.half - quick, quick), (plan.span - quick, quick), (plan.rows - quick, quick)),
+        (0, (quick, plan.half - quick), (quick, plan.span - quick), (quick, plan.span - quick)),
+        (1, (0, plan.half - quick), (0, plan.span - quick), (plan.span, plan.rows - quick - plan.span)),
+    )
+
+    def first_a(p, i):
+        toks, lanes = pl.ds(i * piece, piece), pl.ds(*parts[p][3])
+        return pltpu.make_async_copy(
+            a_ref.at[0, first_m, toks, lanes], a_buf.at[first_m, toks, lanes], first_sem.at[p, i]
+        )
 
     def first_g(i):
-        toks, (m, cols) = pl.ds(i * piece, piece), columns(job_unit(0, 0, 0))
-        return pltpu.make_async_copy(g_ref.at[0, m, toks, cols], g_buf.at[0, 0, toks], first_sem.at[2, i])
-
-    def first_product(d):
+        toks, (m, cols) = pl.ds(i * piece, piece), columns(first_unit)
+        return pltpu.make_async_copy(g_ref.at[0, m, toks, cols], g_buf.at[0, 0, toks], first_sem.at[len(parts), i])
+
+    def first_remote(p):
+        d, (row, tall), _, _ = parts[p]
+        m, cols = columns(first_unit)
+        at = x_ref.at[m, pl.ds(row0[d] + row, tall), cols]
+        return pltpu.make_async_remote_copy(
+            src_ref=at,
+            dst_ref=at,
+            send_sem=first_send.at[p],
+            recv_sem=first_recv.at[p],
+            device_id={axis: neighbours[d]},
+            device_id_type=pl.DeviceIdType.MESH,
+        )
+
+    def first_part(p):
+        d, (row, tall), (at, wide), _ = parts[p]
         for i in range(PIECES):
-            first_a(d, i).wait()
-            if d == 0:
+            first_a(p, i).wait()
+            if p == 0:
                 first_g(i).wait()
             toks = pl.ds(i * piece, piece)
-            part = dot(a_buf[0, toks, pl.ds(lane0[d], plan.span)], g_buf[0, 0, toks])
+            made = dot(a_buf[first_m, toks, pl.ds(lane0[d] + at, wide)], g_buf[0, 0, toks])
             if i == 0:
-                prod[d, 0] = part
+                prod[d, 0, pl.ds(at, wide), :] = made
             else:
-                prod[d, 0] += part
+                prod[d, 0, pl.ds(at, wide), :] += made
+        m, cols = columns(first_unit)
+        mine = prod[d, 0, pl.ds(row0[d] - lane0[d] + row, tall), :]
+        x_ref[m, pl.ds(row0[d] + row, tall), cols] = mine.astype(x_ref.dtype)
+        if p == 0:
+            pl.semaphore_wait(barrier, 2)
+        first_remote(p).start()
+
+    other_a = pltpu.make_async_copy(a_ref.at[0, other_m], a_buf.at[other_m], a_sem.at[1])
 
     def add_product(d, n, u, fresh):
         off = row0[d] - lane0[d]
         mine = prod[d, lax.rem(n, P_SLOTS), pl.ds(off, plan.half), :]
         m, cols = columns(u)
         there = (m, pl.ds(row0[d], plan.half), cols)
-
-        if fresh is True:
-            x_ref[there] = mine.astype(x_ref.dtype)
-            return
 
         @pl.when(fresh)
         def _():
@@ -197,8 +236,14 @@
     def turn_one(d, n):
         s, k, scatter = plan.at(n)
         has, js, jk = plan.job(n)
-
-        @pl.when(n >= 2)
+        mine = [p for p in range(len(parts)) if parts[p][0] == d]
+
+        @pl.when(n == 2)
+        def _():
+            for p in mine:
+                first_remote(p).wait_recv()
+
+        @pl.when(n > 2)
         def _():
             remote(d, 0, n - 2 + SEMS).wait_recv()
 
@@ -206,24 +251,27 @@
         def _():
             add_product(d, n, job_unit(d, js, jk), jk == 0)
 
-        @pl.when(n >= SEMS)
+        @pl.when(n == SEMS)
+        def _():
+            for p in mine:
+                first_remote(p).wait_send()
+
+        @pl.when(n > SEMS)
         def _():
             remote(d, 0, n).wait_send()
 
-        remote(d, s * ring + chunk(d, k, scatter), n).start()
-
-    def first_turn(d):
-        u = job_unit(d, 0, 0)
-        add_product(d, 0, u, True)
-        remote(d, u, 0).start()
+        remote(d, plan.unit(s, chunk(d, k, scatter)), n).start()
 
     def multiply_next(n):
-        for m in range(1, plan.matrices):
-            if m >= 2:
-
-                @pl.when(n == plan.load_slot(m))
-                def _():
-                    a_load(m).start()
+        @pl.when(n == 1)
+        def _():
+            other_a.wait()
+
+        for m in range(2, plan.matrices):
+
+            @pl.when(n == plan.load_slot(m))
+            def _():
+                a_load(m).start()
 
             @pl.when(n + 1 == plan.need_slot(m))
             def _():
@@ -231,19 +279,15 @@
 
         multiply(n + 1)
 
-    for i in range(PIECES):
-        first_a(0, i).start()
-        first_g(i).start()
-    for i in range(PIECES):
-        first_a(1, i).start()
+    for p in range(len(parts)):
+        for i in range(PIECES):
+            first_a(p, i).start()
+            if p == 0:
+                first_g(i).start()
     fetch(1)
-    if plan.matrices > 1:
-        a_load(1).start()
-    first_product(0)
-    pl.semaphore_wait(barrier, 2)
-    first_turn(0)
-    first_product(1)
-    first_turn(1)
+    other_a.start()
+    for p in range(len(parts)):
+        first_part(p)
     fetch(2)
     multiply_next(0)
     fetch(3)
@@ -255,11 +299,12 @@
         fetch(n + 3)
         return 0
 
-    lax.fori_loop(1, plan.slots, body, 0)
-    for n in range(plan.slots - 2, plan.slots):
+    slots = plan.slots
+    lax.fori_loop(1, slots, body, 0)
+    for n in range(slots - 2, slots):
         for d in (0, 1):
             remote(d, 0, n).wait_recv()
-    for n in range(plan.slots - SEMS, plan.slots):
+    for n in range(slots - SEMS, slots):
         for d in (0, 1):
             remote(d, 0, n).wait_send()
 
@@ -297,7 +342,9 @@
                 pltpu.SemaphoreType.DMA((2, G_SLOTS)),
                 pltpu.SemaphoreType.DMA((2, SEMS)),
                 pltpu.SemaphoreType.DMA((2, SEMS)),
-                pltpu.SemaphoreType.DMA((3, PIECES)),
+                pltpu.SemaphoreType.DMA((5, PIECES)),
+                pltpu.SemaphoreType.DMA((4,)),
+                pltpu.SemaphoreType.DMA((4,)),
             ],
             compiler_params=pltpu.CompilerParams(
                 collective_id=0, has_side_effects=True, vmem_limit_bytes=44 * 2**20

time: 365 us -> 366 us (level)
  no operation moved by 1% of the time
where the time goes in v3:
time: 366 us
  Pallas kernels  366 us (100%)
    pallas_call x1, Pallas kernels, device(): pl.pallas_call(functools.partial(reduce_kernel, plan, axis), out_shape=pl...  360 us

profile of v3, /device:TPU:21, one launch (start us, length us, event | category | flops | bytes accessed | tf_op | source)
XLA Modules:
  0.0 366.2 jit_solution(1195722663943077631)
XLA Ops:
  0.0 359.7 %ring_sums.1.x_ref = bf16[4,896,2560]{2,1,0:T(8,128)(2,1)S(1)} custom-call(bf16[1,4,4096,896]{3,2,1,0:T(8,128)(2,1)} %a_ref.1, bf16[1,4,4096,2560]{3,2,1,0:T(8,128)(2,1)} %g_ref.1), custom_call_target="tpu_custom_call" | custom-call | tf_op jit(solution)/shard_map/ring_sums/pallas_call | solution.py:332
  359.8 6.4 %write_sums.1 = bf16[4,896,2560]{2,1,0:T(8,128)(2,1)} custom-call(bf16[4,896,2560]{2,1,0:T(8,128)(2,1)S(1)} %ring_sums.1.x_ref), custom_call_target="tpu_custom_call" | custom-call | tf_op jit(solution)/shard_map/write_sums/pallas_call | solution.py:354

commit v4 on v3

--- a/solution.py
+++ b/solution.py
@@ -34,11 +34,19 @@
         self.span = -(-self.half // LANES) * LANES
         self.phase = 2 * (ring - 1)
         self.slots = self.sets * self.phase
+        self.cut = self.slots - 1
 
     def unit(self, s, c):
         h = self.per_matrix // 2
         pair = jnp.where(c < h, c + h * s, self.per_matrix + c - h + (self.ring - h) * s)
         return jnp.where(s < 2, pair, s * self.ring + c)
+
+    def columns(self, u):
+        j = lax.rem(u, self.per_matrix)
+        return u // self.per_matrix, pl.ds(pl.multiple_of(j * COLS, COLS), COLS)
+
+    def chunk(self, me, d, hop):
+        return lax.rem(me + (self.ring - hop if d == 0 else self.ring - 2 + hop), self.ring)
 
     def final_slot(self, s):
         return (self.phase + 1 + 2 * s) if s < 2 else s * self.phase + 1
@@ -87,7 +95,7 @@
         return has, jnp.where(ends, which, s), jnp.where(ends, self.ring - 1, k)
 
 
-def reduce_kernel(plan, axis, a_ref, g_ref, x_ref, a_buf, g_buf, prod, a_sem, g_sem, send_sem, recv_sem, first_sem, first_send, first_recv):
+def reduce_kernel(plan, axis, a_ref, g_ref, x_ref, r_ref, l_ref, a_buf, g_buf, prod, a_sem, g_sem, send_sem, recv_sem, first_sem, first_send, first_recv):
     ring = plan.ring
     me = lax.axis_index(axis)
     neighbours = (lax.rem(me + 1, ring), lax.rem(me + ring - 1, ring))
@@ -187,12 +195,18 @@
             device_id_type=pl.DeviceIdType.MESH,
         )
 
+    other_a = pltpu.make_async_copy(a_ref.at[0, other_m], a_buf.at[other_m], a_sem.at[1])
+
     def first_part(p):
         d, (row, tall), (at, wide), _ = parts[p]
         for i in range(PIECES):
             first_a(p, i).wait()
             if p == 0:
                 first_g(i).wait()
+            if p + 1 < len(parts):
+                first_a(p + 1, i).start()
+            elif i == 0:
+                other_a.start()
             toks = pl.ds(i * piece, piece)
             made = dot(a_buf[first_m, toks, pl.ds(lane0[d] + at, wide)], g_buf[0, 0, toks])
             if i == 0:
@@ -206,8 +220,6 @@
             pl.semaphore_wait(barrier, 2)
         first_remote(p).start()
 
-    other_a = pltpu.make_async_copy(a_ref.at[0, other_m], a_buf.at[other_m], a_sem.at[1])
-
     def add_product(d, n, u, fresh):
         off = row0[d] - lane0[d]
         mine = prod[d, lax.rem(n, P_SLOTS), pl.ds(off, plan.half), :]
@@ -222,11 +234,13 @@
         def _():
             x_ref[there] = (x_ref[there].astype(jnp.float32) + mine).astype(x_ref.dtype)
 
-    def remote(d, u, n):
+    tails = (r_ref, l_ref)
+
+    def remote(d, u, n, there=None):
         i = lax.rem(n, SEMS)
         return pltpu.make_async_remote_copy(
             src_ref=block(u, d),
-            dst_ref=block(u, d),
+            dst_ref=block(u, d) if there is None else there,
             send_sem=send_sem.at[d, i],
             recv_sem=recv_sem.at[d, i],
             device_id={axis: neighbours[d]},
@@ -260,7 +274,15 @@
         def _():
             remote(d, 0, n).wait_send()
 
-        remote(d, plan.unit(s, chunk(d, k, scatter)), n).start()
+        u = plan.unit(s, chunk(d, k, scatter))
+
+        @pl.when(n != plan.cut - 2)
+        def _():
+            remote(d, u, n).start()
+
+        @pl.when(n == plan.cut - 2)
+        def _():
+            remote(d, u, n, tails[d]).start()
 
     def multiply_next(n):
         @pl.when(n == 1)
@@ -279,14 +301,12 @@
 
         multiply(n + 1)
 
+    for i in range(PIECES):
+        first_a(0, i).start()
+        first_g(i).start()
     for p in range(len(parts)):
-        for i in range(PIECES):
-            first_a(p, i).start()
-            if p == 0:
-                first_g(i).start()
-    fetch(1)
-    other_a.start()
-    for p in range(len(parts)):
+        if p == 3:
+            fetch(1)
         first_part(p)
     fetch(2)
     multiply_next(0)
@@ -299,11 +319,11 @@
         fetch(n + 3)
         return 0
 
-    slots = plan.slots
+    slots = plan.cut
     lax.fori_loop(1, slots, body, 0)
     for n in range(slots - 2, slots):
         for d in (0, 1):
-            remote(d, 0, n).wait_recv()
+            remote(d, 0, n, tails[d] if n == slots - 2 else None).wait_recv()
     for n in range(slots - SEMS, slots):
         for d in (0, 1):
             remote(d, 0, n).wait_send()
@@ -322,6 +342,20 @@
         c.wait()
 
 
+def place_kernel(plan, axis, x_ref, *refs):
+    *blocks, out_ref, sem = refs
+    me = lax.axis_index(axis)
+    copies = []
+    for i, b in enumerate(blocks):
+        d, hop = i % 2, plan.ring - 2 + i // 2
+        m, cols = plan.columns(plan.unit(plan.sets - 1, plan.chunk(me, d, hop)))
+        copies.append(pltpu.make_async_copy(b, out_ref.at[m, pl.ds(d * plan.half, plan.half), cols], sem.at[i]))
+    for c in copies:
+        c.start()
+    for c in copies:
+        c.wait()
+
+
 def solution(mesh):
     axis = "dp"
 
@@ -329,11 +363,20 @@
         _, matrices, tokens, rows = a.shape
         cols = g.shape[-1]
         plan = Plan(mesh.shape[axis], matrices, tokens, rows, cols)
-        sums = pl.pallas_call(
+        block = (plan.half, COLS)
+        sums, right, left = pl.pallas_call(
             functools.partial(reduce_kernel, plan, axis),
-            out_shape=pltpu.VMEM((matrices, rows, cols), jnp.bfloat16),
+            out_shape=(
+                pltpu.VMEM((matrices, rows, cols), jnp.bfloat16),
+                jax.ShapeDtypeStruct(block, jnp.bfloat16),
+                jax.ShapeDtypeStruct(block, jnp.bfloat16),
+            ),
             in_specs=[pl.BlockSpec(memory_space=pl.ANY)] * 2,
-            out_specs=pl.BlockSpec(memory_space=pltpu.VMEM),
+            out_specs=(
+                pl.BlockSpec(memory_space=pltpu.VMEM),
+                pl.BlockSpec(memory_space=pl.ANY),
+                pl.BlockSpec(memory_space=pl.ANY),
+            ),
             scratch_shapes=[
                 pltpu.VMEM((A_SLOTS, tokens, rows), jnp.bfloat16),
                 pltpu.VMEM((2, G_SLOTS, tokens, COLS), jnp.bfloat16),
@@ -351,15 +394,31 @@
             ),
             name="ring_sums",
         )(a, g)
-        return pl.pallas_call(
+        ring = plan.ring
+        from_left = lax.ppermute(right, axis, [(i, (i + 1) % ring) for i in range(ring)])
+        from_right = lax.ppermute(left, axis, [(i, (i - 1) % ring) for i in range(ring)])
+        result = jax.ShapeDtypeStruct((matrices, rows, cols), jnp.bfloat16)
+        size = matrices * rows * cols * 2
+        written = pl.pallas_call(
             functools.partial(write_kernel, WRITES),
-            out_shape=jax.ShapeDtypeStruct((matrices, rows, cols), jnp.bfloat16),
+            out_shape=result,
             in_specs=[pl.BlockSpec(memory_space=pltpu.VMEM)],
             out_specs=pl.BlockSpec(memory_space=pl.ANY),
             scratch_shapes=[pltpu.SemaphoreType.DMA((matrices * WRITES,))],
             compiler_params=pltpu.CompilerParams(vmem_limit_bytes=2**20),
+            cost_estimate=pl.CostEstimate(flops=0, bytes_accessed=2 * size, transcendentals=0),
             name="write_sums",
         )(pltpu.with_memory_space_constraint(sums, pltpu.VMEM))
+        return pl.pallas_call(
+            functools.partial(place_kernel, plan, axis),
+            out_shape=result,
+            in_specs=[pl.BlockSpec(memory_space=pl.ANY)] + [pl.BlockSpec(memory_space=pltpu.VMEM)] * 4,
+            out_specs=pl.BlockSpec(memory_space=pl.ANY),
+            scratch_shapes=[pltpu.SemaphoreType.DMA((4,))],
+            input_output_aliases={0: 0},
+            compiler_params=pltpu.CompilerParams(vmem_limit_bytes=4 * 2**20),
+            name="place_last",
+        )(written, right, left, from_left, from_right)
 
     spec = P(("rep", axis))
     return jax.shard_map(device, mesh=mesh, in_specs=(spec, spec), out_specs=P("rep"), check_vma=False)

time: 366 us -> 366 us (level)
    pallas_call x2 -> x3, Pallas kernels: 366 us -> 363 us  [the longest x1 356 us: device(): pl.pallas_call(functools.partial(reduce_kernel, plan, axis), out_shape=(p...]
  transfers between devices with their start and end apart: 0 -> 2, of which waited for: 0 -> 0; matrix products, arithmetic and copies ran while one was open for 0% -> 0% of each run, Pallas kernels for 0% -> 2%
where the time goes in v4:
time: 366 us
  Pallas kernels  363 us (99%)
    pallas_call x1, Pallas kernels, device(): pl.pallas_call(functools.partial(reduce_kernel, plan, axis), out_shape=(p...  356 us
  transfers between devices with their start and end apart: 2, of which 0 were waited for; matrix products, arithmetic and copies ran while one was open for 0% of the time, Pallas kernels for 2%

profile of v4, /device:TPU:21, one launch (start us, length us, event | category | flops | bytes accessed | tf_op | source)
XLA Modules:
  0.0 365.9 jit_solution(15535527568169323483)
XLA Ops:
  0.0 355.6 %ring_sums.1 = (bf16[4,896,2560]{2,1,0:T(8,128)(2,1)S(1)}, bf16[448,256]{1,0:T(8,128)(2,1)}, bf16[448,256]{1,0:T(8,128)(2,1)}) custom-call(bf16[1,4,4096,896]{3,2,1,0:T(8,128)(2,1)} %a_ref.1, bf16[1,4,4096,2560]{3,2,1,0:T(8,128)(2,1)} %g_ref.1), custom_call_target="tpu_custom_call" | custom-call | tf_op jit(solution)/shard_map/ring_sums/pallas_call | solution.py:367
  355.6 0.1 collective-permute-start
  355.7 2.7 collective-permute-start.1
  358.4 0.0 copy-start
  358.4 0.0 copy-start.1
  358.4 6.4 %write_sums.1.x_ref = bf16[4,896,2560]{2,1,0:T(8,128)(2,1)} custom-call(bf16[4,896,2560]{2,1,0:T(8,128)(2,1)S(1)} %get-tuple-element.8.x_ref), custom_call_target="tpu_custom_call" | custom-call | bytes 36700160 | tf_op jit(solution)/shard_map/write_sums/pallas_call | solution.py:402
  364.8 0.0 collective-permute-done.refs_2_
  364.9 0.0 collective-permute-done.1.refs_3_
  364.9 0.0 copy-done
  364.9 0.0 copy-done.1
  364.9 1.0 place_last.1
Async XLA Ops:
  355.6 9.2 %collective-permute-start = (bf16[448,256]{1,0:T(8,128)(2,1)}, bf16[448,256]{1,0:T(8,128)(2,1)S(1)}, u32[]{:S(2)}, u32[]{:S(2)}) collective-permute-start(bf16[448,256]{1,0:T(8,128)(2,1)} %get-tuple-element.9.refs_0_), channel_id=1, source_target_pairs={{0,1},{1,2},{2,3},{3,4},{4,5},{5,6},{6,7},{7,0},{8,9},{9,10},{10,1... | collective-permute-start | bytes 688136 | tf_op jit(solution)/shard_map/ppermute | solution.py:398
  355.7 9.1 %collective-permute-start.1 = (bf16[448,256]{1,0:T(8,128)(2,1)}, bf16[448,256]{1,0:T(8,128)(2,1)S(1)}, u32[]{:S(2)}, u32[]{:S(2)}) collective-permute-start(bf16[448,256]{1,0:T(8,128)(2,1)} %get-tuple-element.10.refs_1_), channel_id=1, source_target_pairs={{0,7},{1,0},{2,1},{3,2},{4,3},{5,4},{6,5},{7,6},{8,15},{9,8},{10,9... | collective-permute-start | bytes 688136 | tf_op jit(solution)/shard_map/ppermute | solution.py:399
  358.4 6.5 %copy-start = (bf16[448,256]{1,0:T(8,128)(2,1)S(1)}, bf16[448,256]{1,0:T(8,128)(2,1)}, u32[]{:S(2)}) copy-start(bf16[448,256]{1,0:T(8,128)(2,1)} %get-tuple-element.9.refs_0_) | copy-start | bytes 688132
  358.4 6.5 %copy-start.1 = (bf16[448,256]{1,0:T(8,128)(2,1)S(1)}, bf16[448,256]{1,0:T(8,128)(2,1)}, u32[]{:S(2)}) copy-start(bf16[448,256]{1,0:T(8,128)(2,1)} %get-tuple-element.10.refs_1_) | copy-start | bytes 688132

commit v5 on v2

--- a/solution.py
+++ b/solution.py
@@ -32,6 +32,17 @@
         self.span = -(-self.half // LANES) * LANES
         self.phase = 2 * (ring - 1)
         self.slots = self.sets * self.phase
+        self.cut = self.slots - 1
+
+    def unit(self, s, c):
+        return s * self.ring + c
+
+    def columns(self, u):
+        j = lax.rem(u, self.per_matrix)
+        return u // self.per_matrix, pl.ds(pl.multiple_of(j * COLS, COLS), COLS)
+
+    def chunk(self, me, d, hop):
+        return lax.rem(me + (self.ring - hop if d == 0 else self.ring - 2 + hop), self.ring)
 
     def final_slot(self, s):
         return (self.phase + 1 + 2 * s) if s < 2 else s * self.phase + 1
@@ -73,7 +84,7 @@
         return has, jnp.where(ends, which, s), jnp.where(ends, self.ring - 1, k)
 
 
-def reduce_kernel(plan, axis, a_ref, g_ref, x_ref, a_buf, g_buf, prod, a_sem, g_sem, send_sem, recv_sem, first_sem):
+def reduce_kernel(plan, axis, a_ref, g_ref, x_ref, r_ref, l_ref, a_buf, g_buf, prod, a_sem, g_sem, send_sem, recv_sem, first_sem):
     ring = plan.ring
     me = lax.axis_index(axis)
     neighbours = (lax.rem(me + 1, ring), lax.rem(me + ring - 1, ring))
@@ -85,18 +96,15 @@
         pl.semaphore_signal(barrier, inc=1, device_id={axis: there}, device_id_type=pl.DeviceIdType.MESH)
 
     def chunk(d, k, scatter):
-        hop = k + jnp.where(scatter, 1, 0)
-        return lax.rem(me + (ring - hop if d == 0 else ring - 2 + hop), ring)
+        return plan.chunk(me, d, k + jnp.where(scatter, 1, 0))
 
     def shared(k):
         return lax.rem(2 * k, ring) == 0
 
     def job_unit(d, s, k):
-        return s * ring + chunk(d, k, True)
-
-    def columns(u):
-        j = lax.rem(u, plan.per_matrix)
-        return u // plan.per_matrix, pl.ds(pl.multiple_of(j * COLS, COLS), COLS)
+        return plan.unit(s, chunk(d, k, True))
+
+    columns = plan.columns
 
     def block(u, d):
         m, cols = columns(u)
@@ -183,11 +191,13 @@
         def _():
             x_ref[there] = (x_ref[there].astype(jnp.float32) + mine).astype(x_ref.dtype)
 
-    def remote(d, u, n):
+    tails = (r_ref, l_ref)
+
+    def remote(d, u, n, there=None):
         i = lax.rem(n, SEMS)
         return pltpu.make_async_remote_copy(
             src_ref=block(u, d),
-            dst_ref=block(u, d),
+            dst_ref=block(u, d) if there is None else there,
             send_sem=send_sem.at[d, i],
             recv_sem=recv_sem.at[d, i],
             device_id={axis: neighbours[d]},
@@ -210,7 +220,15 @@
         def _():
             remote(d, 0, n).wait_send()
 
-        remote(d, s * ring + chunk(d, k, scatter), n).start()
+        u = plan.unit(s, chunk(d, k, scatter))
+
+        @pl.when(n != plan.cut - 2)
+        def _():
+            remote(d, u, n).start()
+
+        @pl.when(n == plan.cut - 2)
+        def _():
+            remote(d, u, n, tails[d]).start()
 
     def first_turn(d):
         u = job_unit(d, 0, 0)
@@ -239,12 +257,12 @@
     fetch(1)
     if plan.matrices > 1:
         a_load(1).start()
+    fetch(2)
     first_product(0)
     pl.semaphore_wait(barrier, 2)
     first_turn(0)
     first_product(1)
     first_turn(1)
-    fetch(2)
     multiply_next(0)
     fetch(3)
 
@@ -255,11 +273,12 @@
         fetch(n + 3)
         return 0
 
-    lax.fori_loop(1, plan.slots, body, 0)
-    for n in range(plan.slots - 2, plan.slots):
+    slots = plan.cut
+    lax.fori_loop(1, slots, body, 0)
+    for n in range(slots - 2, slots):
         for d in (0, 1):
-            remote(d, 0, n).wait_recv()
-    for n in range(plan.slots - SEMS, plan.slots):
+            remote(d, 0, n, tails[d] if n == slots - 2 else None).wait_recv()
+    for n in range(slots - SEMS, slots):
         for d in (0, 1):
             remote(d, 0, n).wait_send()
 
@@ -277,6 +296,20 @@
         c.wait()
 
 
+def place_kernel(plan, axis, x_ref, *refs):
+    *blocks, out_ref, sem = refs
+    me = lax.axis_index(axis)
+    copies = []
+    for i, b in enumerate(blocks):
+        d, hop = i % 2, plan.ring - 2 + i // 2
+        m, cols = plan.columns(plan.unit(plan.sets - 1, plan.chunk(me, d, hop)))
+        copies.append(pltpu.make_async_copy(b, out_ref.at[m, pl.ds(d * plan.half, plan.half), cols], sem.at[i]))
+    for c in copies:
+        c.start()
+    for c in copies:
+        c.wait()
+
+
 def solution(mesh):
     axis = "dp"
 
@@ -284,11 +317,20 @@
         _, matrices, tokens, rows = a.shape
         cols = g.shape[-1]
         plan = Plan(mesh.shape[axis], matrices, tokens, rows, cols)
-        sums = pl.pallas_call(
+        block = (plan.half, COLS)
+        sums, right, left = pl.pallas_call(
             functools.partial(reduce_kernel, plan, axis),
-            out_shape=pltpu.VMEM((matrices, rows, cols), jnp.bfloat16),
+            out_shape=(
+                pltpu.VMEM((matrices, rows, cols), jnp.bfloat16),
+                jax.ShapeDtypeStruct(block, jnp.bfloat16),
+                jax.ShapeDtypeStruct(block, jnp.bfloat16),
+            ),
             in_specs=[pl.BlockSpec(memory_space=pl.ANY)] * 2,
-            out_specs=pl.BlockSpec(memory_space=pltpu.VMEM),
+            out_specs=(
+                pl.BlockSpec(memory_space=pltpu.VMEM),
+                pl.BlockSpec(memory_space=pl.ANY),
+                pl.BlockSpec(memory_space=pl.ANY),
+            ),
             scratch_shapes=[
                 pltpu.VMEM((A_SLOTS, tokens, rows), jnp.bfloat16),
                 pltpu.VMEM((2, G_SLOTS, tokens, COLS), jnp.bfloat16),
@@ -304,15 +346,31 @@
             ),
             name="ring_sums",
         )(a, g)
-        return pl.pallas_call(
+        ring = plan.ring
+        from_left = lax.ppermute(right, axis, [(i, (i + 1) % ring) for i in range(ring)])
+        from_right = lax.ppermute(left, axis, [(i, (i - 1) % ring) for i in range(ring)])
+        result = jax.ShapeDtypeStruct((matrices, rows, cols), jnp.bfloat16)
+        size = matrices * rows * cols * 2
+        written = pl.pallas_call(
             functools.partial(write_kernel, WRITES),
-            out_shape=jax.ShapeDtypeStruct((matrices, rows, cols), jnp.bfloat16),
+            out_shape=result,
             in_specs=[pl.BlockSpec(memory_space=pltpu.VMEM)],
             out_specs=pl.BlockSpec(memory_space=pl.ANY),
             scratch_shapes=[pltpu.SemaphoreType.DMA((matrices * WRITES,))],
             compiler_params=pltpu.CompilerParams(vmem_limit_bytes=2**20),
+            cost_estimate=pl.CostEstimate(flops=0, bytes_accessed=2 * size, transcendentals=0),
             name="write_sums",
         )(pltpu.with_memory_space_constraint(sums, pltpu.VMEM))
+        return pl.pallas_call(
+            functools.partial(place_kernel, plan, axis),
+            out_shape=result,
+            in_specs=[pl.BlockSpec(memory_space=pl.ANY)] + [pl.BlockSpec(memory_space=pltpu.VMEM)] * 4,
+            out_specs=pl.BlockSpec(memory_space=pl.ANY),
+            scratch_shapes=[pltpu.SemaphoreType.DMA((4,))],
+            input_output_aliases={0: 0},
+            compiler_params=pltpu.CompilerParams(vmem_limit_bytes=4 * 2**20),
+            name="place_last",
+        )(written, right, left, from_left, from_right)
 
     spec = P(("rep", axis))
     return jax.shard_map(device, mesh=mesh, in_specs=(spec, spec), out_specs=P("rep"), check_vma=False)

time: 365 us -> 365 us (level)
  Pallas kernels: 365 us -> 361 us
    pallas_call x2 -> x3, Pallas kernels: 365 us -> 361 us  [the longest x1 354 us: device(): pl.pallas_call(functools.partial(reduce_kernel, plan, axis), out_shape=(p...]
  transfers between devices with their start and end apart: 0 -> 2, of which waited for: 0 -> 0; matrix products, arithmetic and copies ran while one was open for 0% -> 0% of each run, Pallas kernels for 0% -> 2%
where the time goes in v5:
time: 365 us; the launch traced here: 364 us
  Pallas kernels  361 us (99%)
    pallas_call x1, Pallas kernels, device(): pl.pallas_call(functools.partial(reduce_kernel, plan, axis), out_shape=(p...  354 us
  transfers between devices with their start and end apart: 2, of which 0 were waited for; matrix products, arithmetic and copies ran while one was open for 0% of the time, Pallas kernels for 2%

profile of v5, /device:TPU:21, one launch (start us, length us, event | category | flops | bytes accessed | tf_op | source)
XLA Modules:
  0.0 364.2 jit_solution(9027169885219178657)
XLA Ops:
  0.0 353.9 %ring_sums.1 = (bf16[4,896,2560]{2,1,0:T(8,128)(2,1)S(1)}, bf16[448,256]{1,0:T(8,128)(2,1)}, bf16[448,256]{1,0:T(8,128)(2,1)}) custom-call(bf16[1,4,4096,896]{3,2,1,0:T(8,128)(2,1)} %a_ref.1, bf16[1,4,4096,2560]{3,2,1,0:T(8,128)(2,1)} %g_ref.1), custom_call_target="tpu_custom_call" | custom-call | tf_op jit(solution)/shard_map/ring_sums/pallas_call | solution.py:321
  353.9 0.1 collective-permute-start
  354.1 2.7 collective-permute-start.1
  356.7 0.0 copy-start
  356.7 0.0 copy-start.1
  356.7 6.4 %write_sums.1.x_ref = bf16[4,896,2560]{2,1,0:T(8,128)(2,1)} custom-call(bf16[4,896,2560]{2,1,0:T(8,128)(2,1)S(1)} %get-tuple-element.8.x_ref), custom_call_target="tpu_custom_call" | custom-call | bytes 36700160 | tf_op jit(solution)/shard_map/write_sums/pallas_call | solution.py:354
  363.2 0.0 collective-permute-done.refs_2_
  363.2 0.0 collective-permute-done.1.refs_3_
  363.2 0.0 copy-done
  363.2 0.0 copy-done.1
  363.2 1.0 place_last.1
Async XLA Ops:
  353.9 9.2 %collective-permute-start = (bf16[448,256]{1,0:T(8,128)(2,1)}, bf16[448,256]{1,0:T(8,128)(2,1)S(1)}, u32[]{:S(2)}, u32[]{:S(2)}) collective-permute-start(bf16[448,256]{1,0:T(8,128)(2,1)} %get-tuple-element.9.refs_0_), channel_id=1, source_target_pairs={{0,1},{1,2},{2,3},{3,4},{4,5},{5,6},{6,7},{7,0},{8,9},{9,10},{10,1... | collective-permute-start | bytes 688136 | tf_op jit(solution)/shard_map/ppermute | solution.py:350
  354.1 9.1 %collective-permute-start.1 = (bf16[448,256]{1,0:T(8,128)(2,1)}, bf16[448,256]{1,0:T(8,128)(2,1)S(1)}, u32[]{:S(2)}, u32[]{:S(2)}) collective-permute-start(bf16[448,256]{1,0:T(8,128)(2,1)} %get-tuple-element.10.refs_1_), channel_id=1, source_target_pairs={{0,7},{1,0},{2,1},{3,2},{4,3},{5,4},{6,5},{7,6},{8,15},{9,8},{10,9... | collective-permute-start | bytes 688136 | tf_op jit(solution)/shard_map/ppermute | solution.py:351
  356.7 6.5 %copy-start = (bf16[448,256]{1,0:T(8,128)(2,1)S(1)}, bf16[448,256]{1,0:T(8,128)(2,1)}, u32[]{:S(2)}) copy-start(bf16[448,256]{1,0:T(8,128)(2,1)} %get-tuple-element.9.refs_0_) | copy-start | bytes 688132
  356.7 6.5 %copy-start.1 = (bf16[448,256]{1,0:T(8,128)(2,1)S(1)}, bf16[448,256]{1,0:T(8,128)(2,1)}, u32[]{:S(2)}) copy-start(bf16[448,256]{1,0:T(8,128)(2,1)} %get-tuple-element.10.refs_1_) | copy-start | bytes 688132
